TPU v7x, 256 devices: a whole 4x4x8 slice. The times are simulated.
256 devices in a mesh: pairs: 32 (over x, y, core), aux: 8 (over z).
Axes of the slice: x: 4, y: 4, z: 8, core: 2. Of those that a mesh axis runs over, the one named last changes fastest.
Arguments:
- panels: bfloat16 [64, 28672, 256], P(None, ('pairs', 'aux')), may hold values from -0.59765625 to 0.59765625
- domain: int32 [32, 6], replicated, may hold values from 0 to 63, as said below
- pair_slots: int32 [384, 2], P('pairs'), may hold values from 0 to 5
- ranks: int32 [384, 2], P('pairs'), may hold values from 40 to 128
- transforms: bfloat16 [384, 2, 256, 128], P('pairs'), may hold values from -0.375 to 0.375
- trial: bfloat16 [384, 2, 128, 128], P('pairs'), may hold values from -0.5 to 0.5
Outputs:
- sigma: bfloat16 [384, 2, 128, 128], P('pairs', None, 'aux')
Inputs may be any that keep to these rules, and one draw needn't show every extreme that they name: `domain`: each row holds 6 different LMO numbers.
All inputs are finite; a program needn't handle non-finite values.
Results may differ from a plain program's by a relative error of at most 0.0039.
Values may be sent and summed in bfloat16 or wider, within the bound.
A program may use at most 128 MiB of HBM per device.

v0:
```python
import jax
import jax.numpy as jnp
from jax import lax
from jax.sharding import PartitionSpec as P

ROOTS = 2


def cut_along(array, dim, length):
    dims = array.shape
    pieces = array.reshape(*dims[:dim], length, dims[dim] // length, *dims[dim + 1 :])
    return jnp.moveaxis(pieces, dim, 0)


def sum_at_owner(array, axis, dim):
    pieces = cut_along(array, dim, lax.axis_size(axis))
    arrived = lax.all_to_all(pieces, axis, split_axis=0, concat_axis=0, tiled=True)
    return arrived.sum(axis=0)


def per_device(panels, domain, pair_slots, ranks, transforms, trial):
    outgoing = jnp.take(panels, domain.reshape(-1), axis=0)
    received = lax.all_to_all(outgoing, "pairs", split_axis=0, concat_axis=1, tiled=True)
    width = transforms.shape[3]
    positions = lax.broadcasted_iota(jnp.int32, ranks.shape + (width,), 2)
    keep = positions < ranks[:, :, None]
    masked_d = jnp.where(keep[:, :, None, :], transforms, jnp.zeros_like(transforms))
    both_keep = keep[:, :, :, None] & keep[:, :, None, :]
    masked_c = jnp.where(both_keep, trial, jnp.zeros_like(trial)).astype(jnp.float32)

    def one_pair(operands):
        slots, coeffs, amplitude = operands
        left = lax.dynamic_index_in_dim(received, slots[0], 0, keepdims=False)
        right = lax.dynamic_index_in_dim(received, slots[1], 0, keepdims=False)
        left_proj = jnp.dot(left, coeffs, preferred_element_type=jnp.float32).astype(jnp.bfloat16)
        right_proj = jnp.dot(right, coeffs, preferred_element_type=jnp.float32).astype(jnp.bfloat16)
        kmat = jnp.einsum("qa,qb->ab", left_proj, right_proj, preferred_element_type=jnp.float32)
        with_right = jnp.dot(kmat, amplitude, precision=lax.Precision.HIGHEST)
        with_left = jnp.einsum("ac,bc->ab", amplitude, kmat, precision=lax.Precision.HIGHEST)
        return kmat + with_right + with_left

    pieces = []
    for root in range(ROOTS):
        pieces.append(
            sum_at_owner(
                lax.map(one_pair, (pair_slots, masked_d[:, root], masked_c[:, root])), "aux", 1
            )
        )
    summed = jnp.stack(pieces, axis=1)
    return summed.astype(jnp.bfloat16)


def solution(mesh):
    return jax.shard_map(
        per_device,
        mesh=mesh,
        in_specs=(
            P(None, ("pairs", "aux"), None),
            P(),
            P("pairs", None),
            P("pairs", None),
            P("pairs", None, None, None),
            P("pairs", None, None, None),
        ),
        out_specs=P("pairs", None, "aux", None),
        check_vma=False,
    )
```

profile of v0, /device:TPU:12, one launch (start us, length us, event | category | flops | bytes accessed | tf_op | source)
XLA Modules:
  0.0 485.0 jit_solution(10960590465434567596)
XLA Ops:
  1.0 12.5 %gather_fusion = bf16[192,112,256]{2,1,0:T(8,128)(2,1)} fusion(bf16[64,112,256]{2,1,0:T(8,128)(2,1)} %param.10, s32[1024]{0:T(1024)S(1)} %pad_clamp_fusion), kind=kCustom, calls=%fused_computation | custom fusion | bytes 22020864 | tf_op jit(solution)/shard_map/jit(_take)/gather | solution.py:22
  13.5 10.0 %broadcast_select_fusion = bf16[192,112,256]{2,1,0:T(8,128)(2,1)} fusion(bf16[192,112,256]{2,1,0:T(8,128)(2,1)} %gather_fusion, pred[192]{0:T(512)(128)(4,1)S(1)} %compare_and_fusion), kind=kLoop, calls=%fused_computation.51 | loop fusion | flops 5505024 | bytes 22020288 | tf_op jit(solution)/shard_map/jit(_take)/select_n | solution.py:22
  23.4 7.7 %all-to-all-start = ((bf16[192,112,256]{2,1,0:T(8,128)(2,1)}), bf16[192,112,256]{2,1,0:T(8,128)(2,1)}, u32[]{:S(2)}, u32[]{:S(2)}) async-start(bf16[192,112,256]{2,1,0:T(8,128)(2,1)} %broadcast_select_fusion), calls=%async_computation | async-start | bytes 22020096 | tf_op jit(solution)/shard_map/all_to_all | solution.py:23
  33.3 169.6 %all-to-all-done = bf16[192,112,256]{2,1,0:T(8,128)(2,1)} async-done(((bf16[192,112,256]{2,1,0:T(8,128)(2,1)}), bf16[192,112,256]{2,1,0:T(8,128)(2,1)}, u32[]{:S(2)}, u32[]{:S(2)}) %all-to-all-start) | async-done | bytes 11010080 | tf_op jit(solution)/shard_map/all_to_all | solution.py:23
  202.9 9.7 %copy.22 = bf16[32,6,112,256]{3,2,0,1:T(8,128)(2,1)} copy(bf16[32,6,112,256]{3,2,1,0:T(8,128)(2,1)} %bitcast.15) | data formatting | bytes 22020096 | tf_op jit(solution)/shard_map/all_to_all | solution.py:23
  212.6 114.8 %while.20 = (s32[]{:T(128)}, f32[12,128,128]{2,1,0:T(8,128)S(1)}, s32[12,2]{0,1:T(2,128)S(1)}, bf16[6,3584,256]{2,1,0:T(8,128)(2,1)}, bf16[12,256,128]{2,1,0:T(8...) while((s32[]{:T(128)}, f32[12,128,128]{2,1,0:T(8,128)S(1)}, ...), condition=%wide.region_1.2_spmd, body=%wide.region_0.1_spmd.sunk | while | flops 638484480 | bytes 6228177 | solution.py:46
  247.7 2.7 fusion.97
  257.3 2.7 fusion.97
  276.4 2.7 fusion.97
  286.0 2.7 fusion.97
  305.1 2.7 fusion.97
  314.6 2.7 fusion.97
  328.4 8.5 %all-to-all-start.1 = ((f32[8,12,16,128]{3,2,1,0:T(8,128)}), f32[8,12,16,128]{3,2,1,0:T(8,128)S(1)}, u32[]{:S(2)}, u32[]{:S(2)}) async-start(f32[8,12,16,128]{3,2,1,0:T(8,128)} %copy.25), calls=%async_computation.1 | async-start | bytes 1572864 | tf_op jit(solution)/shard_map/all_to_all | solution.py:17
  336.9 116.9 %while.21 = (s32[]{:T(128)}, f32[12,128,128]{2,1,0:T(8,128)S(1)}, s32[12,2]{0,1:T(2,128)S(1)}, bf16[6,3584,256]{2,1,0:T(8,128)(2,1)}, bf16[12,256,128]{2,1,0:T(8...) while((s32[]{:T(128)}, f32[12,128,128]{2,1,0:T(8,128)S(1)}, ...), condition=%wide.region_4.5_spmd, body=%wide.region_3.4_spmd.sunk | while | flops 638484480 | bytes 6228177 | solution.py:46
  353.2 2.7 fusion.110
  362.9 2.7 fusion.110
  372.7 2.7 fusion.110
  392.2 2.7 fusion.110
  401.9 2.7 fusion.110
  421.4 2.7 fusion.110
  431.2 2.7 fusion.110
  450.6 2.7 fusion.110
  454.8 7.2 %all-to-all-start.2 = ((f32[8,12,16,128]{3,2,1,0:T(8,128)}), f32[8,12,16,128]{3,2,1,0:T(8,128)S(1)}, u32[]{:S(2)}, u32[]{:S(2)}) async-start(f32[8,12,16,128]{3,2,1,0:T(8,128)} %copy.26), calls=%async_computation.2 | async-start | bytes 1572864 | tf_op jit(solution)/shard_map/all_to_all | solution.py:17
  462.0 22.2 %all-to-all-done.2 = f32[8,12,16,128]{3,2,1,0:T(8,128)S(1)} async-done(((f32[8,12,16,128]{3,2,1,0:T(8,128)}), f32[8,12,16,128]{3,2,1,0:T(8,128)S(1)}, u32[]{:S(2)}, u32[]{:S(2)}) %all-to-all-start.2) | async-done | bytes 786464 | tf_op jit(solution)/shard_map/all_to_all | solution.py:17
  (157 shorter events, 110.9 us)
Async XLA Ops:
  23.4 7.7 %copy-start.3 = (s32[12,2]{0,1:T(2,128)S(1)}, s32[12,2]{0,1:T(2,128)}, u32[]{:S(2)}) copy-start(s32[12,2]{0,1:T(2,128)} %param.13) | copy-start | bytes 292
  23.4 7.8 %copy-start = (bf16[12,2,256,128]{3,2,1,0:T(8,128)(2,1)S(1)}, bf16[12,2,256,128]{3,2,1,0:T(8,128)(2,1)}, u32[]{:S(2)}) copy-start(bf16[12,2,256,128]{3,2,1,0:T(8,128)(2,1)} %param.14) | copy-start | bytes 4718596
  23.4 179.4 %all-to-all-start = ((bf16[192,112,256]{2,1,0:T(8,128)(2,1)}), bf16[192,112,256]{2,1,0:T(8,128)(2,1)}, u32[]{:S(2)}, u32[]{:S(2)}) async-start(bf16[192,112,256]{2,1,0:T(8,128)(2,1)} %broadcast_select_fusion), calls=%async_computation | async-start | bytes 22020096 | tf_op jit(solution)/shard_map/all_to_all | solution.py:23
  31.1 1.5 copy-start.1
  202.9 9.7 %copy-start.2 = (s32[12,2]{0,1:T(2,128)S(1)}, s32[12,2]{0,1:T(2,128)}, u32[]{:S(2)}) copy-start(s32[12,2]{0,1:T(2,128)} %param.12) | copy-start | bytes 292
  328.4 126.4 %all-to-all-start.1 = ((f32[8,12,16,128]{3,2,1,0:T(8,128)}), f32[8,12,16,128]{3,2,1,0:T(8,128)S(1)}, u32[]{:S(2)}, u32[]{:S(2)}) async-start(f32[8,12,16,128]{3,2,1,0:T(8,128)} %copy.25), calls=%async_computation.1 | async-start | bytes 1572864 | tf_op jit(solution)/shard_map/all_to_all | solution.py:17
  454.8 29.5 %all-to-all-start.2 = ((f32[8,12,16,128]{3,2,1,0:T(8,128)}), f32[8,12,16,128]{3,2,1,0:T(8,128)S(1)}, u32[]{:S(2)}, u32[]{:S(2)}) async-start(f32[8,12,16,128]{3,2,1,0:T(8,128)} %copy.26), calls=%async_computation.2 | async-start | bytes 1572864 | tf_op jit(solution)/shard_map/all_to_all | solution.py:17
where the time goes:
time: 488 us; the launch traced here: 485 us
  waiting for transfers between devices  192 us (39%)
  matrix products  127 us (26%)
  loops' own time  89.2 us (18%)
  local copies, waits for them, and re-layouts  41.9 us (9%)
  starting transfers between devices  23.3 us (5%)
  other arithmetic  11.4 us (2%)
    all_to_all x1, waiting for transfers between devices, per_device(): lax.all_to_all(outgoing, 'pairs', split_axis=0, concat_axis=1, tiled=True)  170 us
    another operation x2, loops' own time, per_device(): lax.map(one_pair, (pair_slots, masked_d[:, root], masked_c[:, root]))  89.2 us
    dot_general x24, matrix products, one_pair(): jnp.einsum('qa,qb->ab', left_proj, right_proj, preferred_element_type=jnp...  64.3 us
    dot_general x24, matrix products, one_pair(): jnp.dot(right, coeffs, preferred_element_type=jnp.float32)  51.3 us
    all_to_all x2, waiting for transfers between devices, sum_at_owner(): lax.all_to_all(pieces, axis, split_axis=0, concat_axis=0, tiled=True)  22.2 us
    all_to_all x2, starting transfers between devices, sum_at_owner(): lax.all_to_all(pieces, axis, split_axis=0, concat_axis=0, tiled=True)  15.7 us
    slice x24, local copies, waits for them, and re-layouts, one_pair(): left = lax.dynamic_index_in_dim(received, slots[0], 0, keepdims=False)  13.5 us
    gather x1, local copies, waits for them, and re-layouts, per_device(): outgoing = jnp.take(panels, domain.reshape(-1), axis=0)  12.5 us
  transfers between devices with their start and end apart: 3, of which 2 were waited for; matrix products, arithmetic and copies ran while one was open for 15% of the time, Pallas kernels for 0%

commit v1 on v0

v1 whole, which is shorter than its diff:
```python
import jax
import jax.numpy as jnp
from jax import lax
from jax.experimental import pallas as pl
from jax.experimental.pallas import tpu as pltpu
from jax.sharding import PartitionSpec as P

MESH = pl.DeviceIdType.MESH
NX, NY, NZ = 4, 4, 8
ROOTS = 2
ORDER = (2, 1, 3, 0)
F32, BF16 = jnp.float32, jnp.bfloat16
TRANS_A = (((0,), (0,)), ((), ()))
TRANS_B = (((1,), (1,)), ((), ()))


def split(value):
    high = value.astype(BF16)
    return high, (value - high.astype(F32)).astype(BF16)


def dot(a, b, dims=(((1,), (0,)), ((), ()))):
    return lax.dot_general(a, b, dims, preferred_element_type=F32)


def kernel(
    domain, ranks, panels, slots_in, transforms, trial, out,
    recv0, recv1, recv2, recv3, stage, slots_v, slots_s,
    gown, gsend1, gsend2, gsend3, grecv1, grecv2, grecv3,
    sig_f, sig_b, zrecv,
    send_sem, recv_sem, slot_send, slot_recv, slot_local, gs_sem, gr_sem, zs_sem, zr_sem,
):
    pairs = out.shape[0]
    rows = panels.shape[1]
    lslot = domain.shape[1]
    recvs = (recv0, recv1, recv2, recv3)
    gsends = (None, gsend1, gsend2, gsend3)
    grecvs = (None, grecv1, grecv2, grecv3)
    pos = lax.axis_index("pairs")
    z = lax.axis_index("aux")
    x, y, c = pos // (2 * NY), (pos // 2) % NY, pos % 2

    def place(x2, y2, c2):
        return (x2 % NX) * (2 * NY) + (y2 % NY) * 2 + c2

    def same(m):
        return x + m * (1 - c), y + m * c, c

    def other(m):
        return x + m * c, y + m * (1 - c), 1 - c

    def other_source(m):
        return x + m * (1 - c), y + m * c, 1 - c

    def peer(r):
        return x + r * c, y + r * (1 - c), c

    def group_of(dest, r):
        x2, y2, c2 = dest
        return place(x2 + r * c2, y2 + r * (1 - c2), c2)

    barrier = pltpu.get_barrier_semaphore()
    greeted = 0
    for target in (
        [(place(*same(m)), z) for m in range(1, 4)]
        + [(place(*other(m)), z) for m in range(4)]
        + [(place(*other_source(m)), z) for m in range(1, 4)]
        + [(place(*peer(r)), z) for r in range(1, 4)]
        + [(pos, (z + k) % NZ) for k in range(1, NZ)]
    ):
        pl.semaphore_signal(barrier, inc=1, device_id=target, device_id_type=MESH)
        greeted += 1

    dests = [(same(m), 2 * m) for m in range(1, 4)] + [(other(m), 2 * m + 1) for m in range(4)]
    dests = [dests[k] for k in (1, 5, 0, 2, 4, 6, 3)]

    def fill(dest, r, k):
        group = group_of(dest, r)

        def body(s, carry):
            stage[k, r, s] = panels[domain[group, s]]
            return carry

        lax.fori_loop(0, lslot, body, 0)

    def panel_copy(dest, block, r, k):
        return pltpu.make_async_remote_copy(
            src_ref=stage.at[k, r],
            dst_ref=recvs[r].at[:, pl.ds(block * rows, rows), :],
            send_sem=send_sem.at[r, k],
            recv_sem=recv_sem.at[r, k],
            device_id=(place(*dest), z),
            device_id_type=MESH,
        )

    def slot_copy(r):
        return pltpu.make_async_remote_copy(
            src_ref=slots_in,
            dst_ref=slots_v.at[r],
            send_sem=slot_send.at[r],
            recv_sem=slot_recv.at[r],
            device_id=(place(*peer(NX - r)), z),
            device_id_type=MESH,
        )

    work = [(r, k) for r in ORDER for k in range(len(dests))]
    fill(dests[0][0], ORDER[0], 0)
    fill(dests[1][0], ORDER[0], 1)
    pl.semaphore_wait(barrier, greeted)
    for r in range(1, 4):
        slot_copy(r).start()
    for n, (r, k) in enumerate(work):
        if n + 2 < len(work):
            r2, k2 = work[n + 2]
            fill(dests[k2][0], r2, k2)
        panel_copy(*dests[k], r, k).start()
    for r in ORDER:
        group = group_of((x, y, c), r)

        def own(s, carry, group=group, r=r):
            recvs[r][s, 0:rows, :] = panels[domain[group, s]]
            return carry

        lax.fori_loop(0, lslot, own, 0)
    for r in range(4):
        if r:
            slot_copy(r).wait()
        local = pltpu.make_async_copy(slots_v.at[r] if r else slots_in, slots_s.at[r], slot_local.at[r])
        local.start()
        local.wait()

    half = pairs // 2

    def g_copy(r, h):
        part = pl.ds(h * half, half)
        return pltpu.make_async_remote_copy(
            src_ref=gsends[r].at[part],
            dst_ref=grecvs[r].at[part],
            send_sem=gs_sem.at[r, h],
            recv_sem=gr_sem.at[r, h],
            device_id=(place(*peer(r)), z),
            device_id_type=MESH,
        )

    def gram(r, p):
        left = recvs[r][slots_s[r, 0, 2 * p]]
        right = recvs[r][slots_s[r, 0, 2 * p + 1]]
        return dot(left, right, TRANS_A)

    for r in ORDER:
        for k in range(len(dests)):
            panel_copy(*dests[k], r, k).wait_recv()
        if r:
            for h in range(2):
                def send_body(p, carry, r=r):
                    gsends[r][p] = gram(r, p).astype(BF16)
                    return carry

                lax.fori_loop(h * half, (h + 1) * half, send_body, 0)
                g_copy(r, h).start()
        else:
            def own_body(p, carry):
                gown[p] = gram(0, p)
                return carry

            lax.fori_loop(0, pairs, own_body, 0)

    def z_copy(k, h):
        part = pl.ds(h * half, half)
        to = (z + k) % NZ
        piece = out.shape[2]
        return pltpu.make_async_remote_copy(
            src_ref=sig_b.at[part, :, pl.ds(pl.multiple_of(to * piece, piece), piece), :],
            dst_ref=zrecv.at[k, part],
            send_sem=zs_sem.at[k, h],
            recv_sem=zr_sem.at[k, h],
            device_id=(pos, to),
            device_id_type=MESH,
        )

    rank = trial.shape[3]
    row_at = lax.broadcasted_iota(jnp.int32, (rank, rank), 0)
    col_at = lax.broadcasted_iota(jnp.int32, (rank, rank), 1)
    for h in range(2):
        for r in range(1, 4):
            g_copy(r, h).wait_recv()

        def sigma_body(p, carry):
            total = gown[p]
            for r in range(1, 4):
                total = total + grecvs[r][p].astype(F32)
            coeffs = jnp.concatenate([transforms[p, 0], transforms[p, 1]], axis=1)
            g_high, g_low = split(total)
            t = dot(g_high, coeffs) + dot(g_low, coeffs)
            t_high, t_low = split(t)
            for root in range(ROOTS):
                cols = slice(root * rank, (root + 1) * rank)
                d = transforms[p, root]
                keep = (row_at < ranks[p, root]) & (col_at < ranks[p, root])
                kmat = dot(d, t_high[:, cols], TRANS_A) + dot(d, t_low[:, cols], TRANS_A)
                kmat = jnp.where(keep, kmat, 0.0)
                amp = jnp.where(keep, trial[p, root].astype(F32), 0.0).astype(BF16)
                k_high, k_low = split(kmat)
                sig = kmat + (dot(k_high, amp) + dot(k_low, amp))
                sig = sig + (dot(amp, k_high, TRANS_B) + dot(amp, k_low, TRANS_B))
                sig_f[p, root] = sig
                sig_b[p, root] = sig.astype(BF16)
            return carry

        lax.fori_loop(h * half, (h + 1) * half, sigma_body, 0)
        for k in (4, 3, 5, 2, 6, 1, 7):
            z_copy(k, h).start()

    piece = out.shape[2]
    for h in range(2):
        for k in range(1, NZ):
            z_copy(k, h).wait_recv()

        def sum_body(p, carry):
            for root in range(ROOTS):
                total = sig_f[p, root, pl.ds(pl.multiple_of(z * piece, piece), piece), :]
                for k in range(1, NZ):
                    total = total + zrecv[k, p, root].astype(F32)
                out[p, root] = total.astype(BF16)
            return carry

        lax.fori_loop(h * half, (h + 1) * half, sum_body, 0)

    for r in ORDER:
        for k in range(len(dests)):
            panel_copy(*dests[k], r, k).wait_send()
    for h in range(2):
        for r in range(1, 4):
            g_copy(r, h).wait_send()
        for k in range(1, NZ):
            z_copy(k, h).wait_send()


def per_device(panels, domain, pair_slots, ranks, transforms, trial):
    pairs, roots, width, rank = transforms.shape
    rows, lslot = panels.shape[1], domain.shape[1]
    flat = pair_slots.reshape(1, -1)
    slots_in = jnp.pad(flat, ((0, 7), (0, 128 - flat.shape[1])))
    smem = pl.BlockSpec(memory_space=pltpu.SMEM)
    vmem = pl.BlockSpec(memory_space=pltpu.VMEM)
    dma = pltpu.SemaphoreType.DMA
    return pl.pallas_call(
        kernel,
        name="sigma",
        out_shape=jax.ShapeDtypeStruct((pairs, roots, rank // NZ, rank), BF16),
        in_specs=[smem, smem, vmem, vmem, vmem, vmem],
        out_specs=vmem,
        scratch_shapes=[pltpu.VMEM((lslot, 8 * rows, width), BF16)] * 4
        + [
            pltpu.VMEM((7, 4, lslot, rows, width), BF16),
            pltpu.VMEM((4, 8, 128), jnp.int32),
            pltpu.SMEM((4, 8, 128), jnp.int32),
            pltpu.VMEM((pairs, width, width), F32),
        ]
        + [pltpu.VMEM((pairs, width, width), BF16)] * 6
        + [
            pltpu.VMEM((pairs, roots, rank, rank), F32),
            pltpu.VMEM((pairs, roots, rank, rank), BF16),
            pltpu.VMEM((NZ, pairs, roots, rank // NZ, rank), BF16),
            dma((4, 7)),
            dma((4, 7)),
            dma((4,)),
            dma((4,)),
            dma((4,)),
            dma((4, 2)),
            dma((4, 2)),
            dma((NZ, 2)),
            dma((NZ, 2)),
        ],
        compiler_params=pltpu.CompilerParams(
            collective_id=0, has_side_effects=True, vmem_limit_bytes=63 * 2**20
        ),
    )(domain, ranks, panels, slots_in, transforms, trial)


def solution(mesh):
    return jax.shard_map(
        per_device,
        mesh=mesh,
        in_specs=(
            P(None, ("pairs", "aux"), None),
            P(),
            P("pairs", None),
            P("pairs", None),
            P("pairs", None, None, None),
            P("pairs", None, None, None),
        ),
        out_specs=P("pairs", None, "aux", None),
        check_vma=False,
    )
```

time: 488 us -> 132 us (0.27)
  the two profiles are of different devices: /device:TPU:12 before, /device:TPU:1 now
where the time goes in v1:
time: 132 us
  Pallas kernels  126 us (95%)
  local copies, waits for them, and re-layouts  5.72 us (4%)
    pallas_call x1, Pallas kernels, per_device(): pl.pallas_call(kernel, name='sigma', out_shape=jax.ShapeDtypeStruct((pair...  126 us
    unnamed x4, local copies, waits for them, and re-layouts  5.03 us

profile of v1, /device:TPU:1, one launch (start us, length us, event | category | flops | bytes accessed | tf_op | source)
XLA Modules:
  0.0 131.5 jit_solution(7382076699641034518)
XLA Ops:
  0.0 0.8 copy.10
  0.8 0.1 reshape.3
  0.9 0.6 pad.4.slots_in
  1.5 1.4 %copy.12.ranks = s32[12,2]{1,0:T(8,128)} copy(s32[12,2]{0,1:T(2,128)} %param.9) | data formatting | bytes 192 | tf_op args[3]
  2.8 1.4 %copy.11.domain = s32[32,6]{1,0:T(8,128)} copy(s32[32,6]{0,1:T(8,128)} %param.7) | data formatting | bytes 1536 | tf_op args[1]
  4.2 125.8 %sigma.1 = bf16[12,2,16,128]{3,2,1,0:T(8,128)(2,1)} custom-call(s32[32,6]{1,0:T(8,128)} %copy.11.domain, s32[12,2]{1,0:T(8,128)} %copy.12.ranks, bf16[64,112,256]{2,1,0:T(8,128)(2,1)} %panels.1, s32[8,128]{1,0:T(8,128)} %pad.4.slots_in, bf16[12,2,256,128]{3,2,1,0:T(8,128)(2,1)} %transforms.1, bf16[12,2,128,128]{3,2,1,0:T(8,128)(2,1)} %trial.1), custom_call_target="tpu_custom_call" | custom-call | tf_op jit(solution)/shard_map/sigma/pallas_call | solution.py:247
  130.0 1.5 %copy.14 = bf16[12,2,16,128]{3,2,1,0:T(8,128)(2,1)} copy(bf16[12,2,16,128]{3,2,1,0:T(8,128)(2,1)} %sigma.1) | data formatting | bytes 196608

commit v2 on v1

v2 whole, which is shorter than its diff:
```python
import jax
import jax.numpy as jnp
from jax import lax
from jax.experimental import pallas as pl
from jax.experimental.pallas import tpu as pltpu
from jax.sharding import PartitionSpec as P

MESH = pl.DeviceIdType.MESH
NX, NY, NZ = 4, 4, 8
ROOTS = 2
ORDER = (2, 1, 3, 0)
CHUNKS = 4
F32, BF16 = jnp.float32, jnp.bfloat16
PLAIN = (((1,), (0,)), ((), ()))
TRANS_A = (((0,), (0,)), ((), ()))
TRANS_B = (((1,), (1,)), ((), ()))


def split(value):
    high = value.astype(BF16)
    return high, (value - high.astype(F32)).astype(BF16)


def dot(a, b, dims=PLAIN):
    return lax.dot_general(a, b, dims, preferred_element_type=F32)


def kernel(
    domain, ranks, slots_in, panels_in, transforms_in, trial_in, out,
    panels, transforms, trial,
    recv0, recv1, recv2, recv3, stage, slots_v, slots_s, dall, gram,
    kown, ksend, krecv, sig_f, sig_b, zrecv,
    in_sem, send_sem, recv_sem, slot_send, slot_recv, slot_local,
    ds_sem, dr_sem, rs_sem, rr_sem, ls_sem, lr_sem,
    ks_sem, kr_sem, zs_sem, zr_sem,
):
    pairs, piece, rank = out.shape[0], out.shape[2], out.shape[3]
    rows = panels.shape[1]
    lslot = domain.shape[0]
    width = transforms.shape[1]
    recvs = (recv0, recv1, recv2, recv3)
    pos = lax.axis_index("pairs")
    z = lax.axis_index("aux")
    x, y, c = pos // (2 * NY), (pos // 2) % NY, pos % 2

    loads = [
        pltpu.make_async_copy(src, dst, in_sem.at[n])
        for n, (src, dst) in enumerate(
            ((panels_in, panels), (transforms_in, transforms), (trial_in, trial))
        )
    ]
    for load in loads:
        load.start()

    def place(x2, y2, c2):
        return (x2 % NX) * (2 * NY) + (y2 % NY) * 2 + c2

    def same(m):
        return x + m * (1 - c), y + m * c, c

    def other(m):
        return x + m * c, y + m * (1 - c), 1 - c

    def other_source(m):
        return x + m * (1 - c), y + m * c, 1 - c

    def peer(r):
        return x + r * c, y + r * (1 - c), c

    def group_of(dest, r):
        x2, y2, c2 = dest
        return place(x2 + r * c2, y2 + r * (1 - c2), c2)

    barrier = pltpu.get_barrier_semaphore()
    greeted = 0
    for target in (
        [(place(*same(m)), z) for m in range(1, 4)]
        + [(place(*other(m)), z) for m in range(4)]
        + [(place(*other_source(m)), z) for m in range(1, 4)]
        + [(place(*peer(r)), z) for r in range(1, 4)]
        + [(pos, (z + k) % NZ) for k in range(1, NZ)]
    ):
        pl.semaphore_signal(barrier, inc=1, device_id=target, device_id_type=MESH)
        greeted += 1

    dests = [(same(m), 2 * m) for m in range(1, 4)] + [(other(m), 2 * m + 1) for m in range(4)]
    dests = [dests[k] for k in (1, 5, 0, 2, 4, 6, 3)]

    def fill(dest, r, k):
        group = group_of(dest, r)
        for s in range(lslot):
            stage[k, r, s] = panels[domain[s, group]]

    def panel_copy(dest, block, r, k):
        return pltpu.make_async_remote_copy(
            src_ref=stage.at[k, r],
            dst_ref=recvs[r].at[:, pl.ds(block * rows, rows), :],
            send_sem=send_sem.at[r, k],
            recv_sem=recv_sem.at[r, k],
            device_id=(place(*dest), z),
            device_id_type=MESH,
        )

    def slot_copy(r):
        return pltpu.make_async_remote_copy(
            src_ref=slots_in,
            dst_ref=slots_v.at[r],
            send_sem=slot_send.at[r],
            recv_sem=slot_recv.at[r],
            device_id=(place(*peer(NX - r)), z),
            device_id_type=MESH,
        )

    part = width // NZ

    def part_of(origin):
        return pl.ds(pl.multiple_of((origin % NZ) * part, part), part)

    def d_copy(r):
        return pltpu.make_async_remote_copy(
            src_ref=transforms.at[:, part_of(z), :],
            dst_ref=dall.at[r - 1, :, part_of(z), :],
            send_sem=ds_sem.at[r],
            recv_sem=dr_sem.at[r],
            device_id=(place(*peer(NX - r)), z),
            device_id_type=MESH,
        )

    def ring_copy(way, step):
        origin = part_of(z - way * step + NZ)
        chosen = slice(None)
        if step == NZ // 2 - 1:
            chosen = pl.ds(0, 2) if way == 1 else pl.ds(2, 1)
        send, recv = (rs_sem, rr_sem) if way == 1 else (ls_sem, lr_sem)
        ref = dall.at[chosen, :, origin, :]
        return pltpu.make_async_remote_copy(
            src_ref=ref,
            dst_ref=ref,
            send_sem=send.at[step],
            recv_sem=recv.at[step],
            device_id=(pos, (z + way + NZ) % NZ),
            device_id_type=MESH,
        )

    def ring(step):
        for way in (1, -1):
            if step:
                ring_copy(way, step - 1).wait_recv()
            if step < NZ // 2:
                ring_copy(way, step).start()

    work = [(r, k) for r in ORDER for k in range(len(dests))]
    loads[0].wait()
    fill(dests[0][0], ORDER[0], 0)
    fill(dests[1][0], ORDER[0], 1)
    loads[1].wait()
    pl.semaphore_wait(barrier, greeted)
    for r in (2, 1, 3):
        d_copy(r).start()
    for r in range(1, 4):
        slot_copy(r).start()
    for n, (r, k) in enumerate(work):
        if n + 2 < len(work):
            r2, k2 = work[n + 2]
            fill(dests[k2][0], r2, k2)
        panel_copy(*dests[k], r, k).start()
    for r in ORDER:
        group = group_of((x, y, c), r)
        for s in range(lslot):
            recvs[r][s, 0:rows, :] = panels[domain[s, group]]
    for r in range(1, 4):
        d_copy(r).wait_recv()
    ring(0)
    for r in range(4):
        if r:
            slot_copy(r).wait()
        local = pltpu.make_async_copy(slots_v.at[r] if r else slots_in, slots_s.at[r], slot_local.at[r])
        local.start()
        local.wait()
    loads[2].wait()

    def wait_panels(r):
        for k in range(len(dests)):
            panel_copy(*dests[k], r, k).wait_recv()

    def grams(r):
        def body(p, carry):
            left = recvs[r][slots_s[r, 0, p]]
            right = recvs[r][slots_s[r, 1, p]]
            gram[r, p] = dot(left, right, TRANS_A)
            return carry

        lax.fori_loop(0, pairs, body, 0)

    def k_of(r, p, d0, d1):
        g_high, g_low = split(gram[r, p])
        coeffs = jnp.concatenate([d0, d1], axis=1)
        t_high, t_low = split(dot(g_high, coeffs) + dot(g_low, coeffs))
        result = []
        for root, d in enumerate((d0, d1)):
            cols = slice(root * rank, (root + 1) * rank)
            both = jnp.concatenate([t_high[:, cols], t_low[:, cols]], axis=1)
            summed = dot(d, both, TRANS_A)
            result.append(summed[:, :rank] + summed[:, rank:])
        return result

    per = pairs // CHUNKS

    def k_copy(r, h):
        some = pl.ds(h * per, per)
        return pltpu.make_async_remote_copy(
            src_ref=ksend.at[r - 1, some],
            dst_ref=krecv.at[r - 1, some],
            send_sem=ks_sem.at[r - 1, h],
            recv_sem=kr_sem.at[r - 1, h],
            device_id=(place(*peer(r)), z),
            device_id_type=MESH,
        )

    wait_panels(2)
    ring(1)
    grams(2)
    ring(2)
    wait_panels(1)
    grams(1)
    ring(3)
    wait_panels(3)
    grams(3)
    ring(4)

    def k_chunk(h, carry):
        for r in (2, 1, 3):
            for n in range(per):
                p = h * per + n
                mats = k_of(r, p, dall[r - 1, ROOTS * p], dall[r - 1, ROOTS * p + 1])
                for root in range(ROOTS):
                    ksend[r - 1, p, root] = mats[root].astype(BF16)
        for r in (2, 1, 3):
            k_copy(r, h).start()
        return carry

    lax.fori_loop(0, CHUNKS, k_chunk, 0)
    wait_panels(0)
    grams(0)

    def own_chunk(h, carry):
        for n in range(per):
            p = h * per + n
            mats = k_of(0, p, transforms[ROOTS * p], transforms[ROOTS * p + 1])
            for root in range(ROOTS):
                kown[p, root] = mats[root]
        return carry

    lax.fori_loop(0, CHUNKS, own_chunk, 0)

    def z_copy(k, h):
        some = pl.ds(h * per, per)
        to = (z + k) % NZ
        return pltpu.make_async_remote_copy(
            src_ref=sig_b.at[some, :, pl.ds(pl.multiple_of(to * piece, piece), piece), :],
            dst_ref=zrecv.at[k, some],
            send_sem=zs_sem.at[k, h],
            recv_sem=zr_sem.at[k, h],
            device_id=(pos, to),
            device_id_type=MESH,
        )

    row_at = lax.broadcasted_iota(jnp.int32, (rank, rank), 0)
    col_at = lax.broadcasted_iota(jnp.int32, (rank, rank), 1)

    def sigma_chunk(h, carry):
        for r in range(1, 4):
            k_copy(r, h).wait_recv()
        for n in range(per):
            p = h * per + n
            for root in range(ROOTS):
                kmat = kown[p, root]
                for r in range(1, 4):
                    kmat = kmat + krecv[r - 1, p, root].astype(F32)
                keep = (row_at < ranks[root, p]) & (col_at < ranks[root, p])
                kmat = jnp.where(keep, kmat, 0.0)
                amp = jnp.where(keep, trial[p, root].astype(F32), 0.0).astype(BF16)
                both = jnp.concatenate(split(kmat), axis=1)
                sig = kmat + dot(both, jnp.concatenate([amp, amp], axis=0))
                sig = sig + dot(jnp.concatenate([amp, amp], axis=1), both, TRANS_B)
                sig_f[p, root] = sig
                sig_b[p, root] = sig.astype(BF16)
        for k in (4, 3, 5, 2, 6, 1, 7):
            z_copy(k, h).start()
        return carry

    lax.fori_loop(0, CHUNKS, sigma_chunk, 0)

    def sum_chunk(h, carry):
        for k in range(1, NZ):
            z_copy(k, h).wait_recv()
        for n in range(per):
            p = h * per + n
            for root in range(ROOTS):
                total = sig_f[p, root, pl.ds(pl.multiple_of(z * piece, piece), piece), :]
                for k in range(1, NZ):
                    total = total + zrecv[k, p, root].astype(F32)
                out[p, root] = total.astype(BF16)
        return carry

    lax.fori_loop(0, CHUNKS, sum_chunk, 0)

    for r in ORDER:
        for k in range(len(dests)):
            panel_copy(*dests[k], r, k).wait_send()
    for r in range(1, 4):
        d_copy(r).wait_send()
    for step in range(NZ // 2):
        for way in (1, -1):
            ring_copy(way, step).wait_send()
    for h in range(CHUNKS):
        for r in range(1, 4):
            k_copy(r, h).wait_send()
        for k in range(1, NZ):
            z_copy(k, h).wait_send()


def per_device(panels, domain, pair_slots, ranks, transforms, trial):
    pairs, roots, width, rank = transforms.shape
    occ, rows, _ = panels.shape
    lslot = domain.shape[1]
    smem = pl.BlockSpec(memory_space=pltpu.SMEM)
    vmem = pl.BlockSpec(memory_space=pltpu.VMEM)
    far = pl.BlockSpec(memory_space=pl.ANY)
    dma = pltpu.SemaphoreType.DMA
    return pl.pallas_call(
        kernel,
        name="sigma",
        out_shape=jax.ShapeDtypeStruct((pairs, roots, rank // NZ, rank), BF16),
        in_specs=[smem, smem, vmem, far, far, far],
        out_specs=vmem,
        scratch_shapes=[
            pltpu.VMEM((occ, rows, width), BF16),
            pltpu.VMEM((pairs * roots, width, rank), BF16),
            pltpu.VMEM((pairs, roots, rank, rank), BF16),
        ]
        + [pltpu.VMEM((lslot, 8 * rows, width), BF16)] * 4
        + [
            pltpu.VMEM((7, 4, lslot, rows, width), BF16),
            pltpu.VMEM((4, 2, pairs), jnp.int32),
            pltpu.SMEM((4, 2, pairs), jnp.int32),
            pltpu.VMEM((3, pairs * roots, width, rank), BF16),
            pltpu.VMEM((4, pairs, width, width), F32),
            pltpu.VMEM((pairs, roots, rank, rank), F32),
            pltpu.VMEM((3, pairs, roots, rank, rank), BF16),
            pltpu.VMEM((3, pairs, roots, rank, rank), BF16),
            pltpu.VMEM((pairs, roots, rank, rank), F32),
            pltpu.VMEM((pairs, roots, rank, rank), BF16),
            pltpu.VMEM((NZ, pairs, roots, rank // NZ, rank), BF16),
            dma((3,)),
            dma((4, 7)),
            dma((4, 7)),
            dma((4,)),
            dma((4,)),
            dma((4,)),
            dma((4,)),
            dma((4,)),
            dma((4,)),
            dma((4,)),
            dma((4,)),
            dma((4,)),
            dma((3, CHUNKS)),
            dma((3, CHUNKS)),
            dma((NZ, CHUNKS)),
            dma((NZ, CHUNKS)),
        ],
        compiler_params=pltpu.CompilerParams(
            collective_id=0, has_side_effects=True, vmem_limit_bytes=67043328
        ),
    )(
        domain.T,
        ranks.T,
        pair_slots.T,
        panels,
        transforms.reshape(pairs * roots, width, rank),
        trial,
    )


def solution(mesh):
    return jax.shard_map(
        per_device,
        mesh=mesh,
        in_specs=(
            P(None, ("pairs", "aux"), None),
            P(),
            P("pairs", None),
            P("pairs", None),
            P("pairs", None, None, None),
            P("pairs", None, None, None),
        ),
        out_specs=P("pairs", None, "aux", None),
        check_vma=False,
    )
```

time: 132 us -> 120 us (0.909)
  Pallas kernels: 126 us -> 118 us
  local copies, waits for them, and re-layouts: 5.72 us -> 1.54 us
    pallas_call x1, Pallas kernels: 126 us -> 118 us  [per_device(): pl.pallas_call(kernel, name='sigma', out_shape=jax.ShapeDtypeStruct((pair...]
    unnamed x4 -> x1, local copies, waits for them, and re-layouts: 5.03 us -> 1.54 us
where the time goes in v2:
time: 120 us; the launch traced here: 119 us
  Pallas kernels  118 us (98%)
  local copies, waits for them, and re-layouts  1.54 us (1%)
    pallas_call x1, Pallas kernels, per_device(): pl.pallas_call(kernel, name='sigma', out_shape=jax.ShapeDtypeStruct((pair...  118 us

profile of v2, /device:TPU:1, one launch (start us, length us, event | category | flops | bytes accessed | tf_op | source)
XLA Modules:
  0.0 119.4 jit_solution(13044074264584982733)
XLA Ops:
  0.0 117.8 %sigma.1 = bf16[12,2,16,128]{3,2,1,0:T(8,128)(2,1)} custom-call(s32[6,32]{1,0:T(8,128)} %bitcast.5, s32[2,12]{1,0:T(2,128)} %bitcast.6, s32[2,12]{1,0:T(2,128)} %bitcast.7, bf16[64,112,256]{2,1,0:T(8,128)(2,1)} %panels_in.1, bf16[24,256,128]{2,1,0:T(8,128)(2,1)} %bitcast.4, bf16[12,2,128,128]{3,2,1,0:T(8,128)(2,1)} %trial_in.1), custom_call_target="tpu_custom_call" | custom-call | tf_op jit(solution)/shard_map/sigma/pallas_call | solution.py:331
  117.8 1.5 %copy.8 = bf16[12,2,16,128]{3,2,1,0:T(8,128)(2,1)} copy(bf16[12,2,16,128]{3,2,1,0:T(8,128)(2,1)} %sigma.1) | data formatting | bytes 196608

commit v3 on v2

--- a/solution.py
+++ b/solution.py
@@ -9,7 +9,8 @@
 NX, NY, NZ = 4, 4, 8
 ROOTS = 2
 ORDER = (2, 1, 3, 0)
-CHUNKS = 4
+CHUNKS = 6
+UNROLL = 3
 F32, BF16 = jnp.float32, jnp.bfloat16
 PLAIN = (((1,), (0,)), ((), ()))
 TRANS_A = (((0,), (0,)), ((), ()))
@@ -78,7 +79,7 @@
         + [(place(*other(m)), z) for m in range(4)]
         + [(place(*other_source(m)), z) for m in range(1, 4)]
         + [(place(*peer(r)), z) for r in range(1, 4)]
-        + [(pos, (z + k) % NZ) for k in range(1, NZ)]
+        + [(pos, (z + k) % NZ) for k in (1, NZ - 1)]
     ):
         pl.semaphore_signal(barrier, inc=1, device_id=target, device_id_type=MESH)
         greeted += 1
@@ -126,56 +127,64 @@
             device_id_type=MESH,
         )
 
-    def ring_copy(way, step):
+    half = pairs * ROOTS // 2
+
+    def ring_copy(way, step, h):
         origin = part_of(z - way * step + NZ)
         chosen = slice(None)
         if step == NZ // 2 - 1:
             chosen = pl.ds(0, 2) if way == 1 else pl.ds(2, 1)
         send, recv = (rs_sem, rr_sem) if way == 1 else (ls_sem, lr_sem)
-        ref = dall.at[chosen, :, origin, :]
+        ref = dall.at[chosen, pl.ds(h * half, half), origin, :]
         return pltpu.make_async_remote_copy(
             src_ref=ref,
             dst_ref=ref,
-            send_sem=send.at[step],
-            recv_sem=recv.at[step],
+            send_sem=send.at[step, h],
+            recv_sem=recv.at[step, h],
             device_id=(pos, (z + way + NZ) % NZ),
             device_id_type=MESH,
         )
 
-    def ring(step):
+    def ring(step, h):
         for way in (1, -1):
             if step:
-                ring_copy(way, step - 1).wait_recv()
+                ring_copy(way, step - 1, h).wait_recv()
             if step < NZ // 2:
-                ring_copy(way, step).start()
+                ring_copy(way, step, h).start()
 
     work = [(r, k) for r in ORDER for k in range(len(dests))]
-    loads[0].wait()
-    fill(dests[0][0], ORDER[0], 0)
-    fill(dests[1][0], ORDER[0], 1)
     loads[1].wait()
     pl.semaphore_wait(barrier, greeted)
     for r in (2, 1, 3):
         d_copy(r).start()
     for r in range(1, 4):
         slot_copy(r).start()
-    for n, (r, k) in enumerate(work):
-        if n + 2 < len(work):
-            r2, k2 = work[n + 2]
-            fill(dests[k2][0], r2, k2)
-        panel_copy(*dests[k], r, k).start()
+    loads[0].wait()
+    for r, k in work:
+        fill(dests[k][0], r, k)
+    for r, k in work:
+        if dests[k][1] % 2:
+            panel_copy(*dests[k], r, k).start()
     for r in ORDER:
         group = group_of((x, y, c), r)
         for s in range(lslot):
             recvs[r][s, 0:rows, :] = panels[domain[s, group]]
     for r in range(1, 4):
         d_copy(r).wait_recv()
-    ring(0)
+    ring(0, 0)
+    ring(0, 1)
+    for r, k in work:
+        if dests[k][1] % 2 == 0:
+            panel_copy(*dests[k], r, k).start()
+    locals_ = [
+        pltpu.make_async_copy(slots_v.at[r] if r else slots_in, slots_s.at[r], slot_local.at[r])
+        for r in range(4)
+    ]
     for r in range(4):
         if r:
             slot_copy(r).wait()
-        local = pltpu.make_async_copy(slots_v.at[r] if r else slots_in, slots_s.at[r], slot_local.at[r])
-        local.start()
+        locals_[r].start()
+    for local in locals_:
         local.wait()
     loads[2].wait()
 
@@ -183,14 +192,18 @@
         for k in range(len(dests)):
             panel_copy(*dests[k], r, k).wait_recv()
 
+    def gram_of(r, p):
+        left = recvs[r][slots_s[r, 0, p]]
+        right = recvs[r][slots_s[r, 1, p]]
+        gram[r, p] = dot(left, right, TRANS_A)
+
     def grams(r):
-        def body(p, carry):
-            left = recvs[r][slots_s[r, 0, p]]
-            right = recvs[r][slots_s[r, 1, p]]
-            gram[r, p] = dot(left, right, TRANS_A)
+        def body(n, carry):
+            for u in range(UNROLL):
+                gram_of(r, n * UNROLL + u)
             return carry
 
-        lax.fori_loop(0, pairs, body, 0)
+        lax.fori_loop(0, pairs // UNROLL, body, 0)
 
     def k_of(r, p, d0, d1):
         g_high, g_low = split(gram[r, p])
@@ -217,58 +230,63 @@
             device_id_type=MESH,
         )
 
-    wait_panels(2)
-    ring(1)
-    grams(2)
-    ring(2)
-    wait_panels(1)
-    grams(1)
-    ring(3)
-    wait_panels(3)
-    grams(3)
-    ring(4)
-
-    def k_chunk(h, carry):
-        for r in (2, 1, 3):
+    def k_part(r, h):
+        def body(chunk, carry):
             for n in range(per):
-                p = h * per + n
+                p = chunk * per + n
                 mats = k_of(r, p, dall[r - 1, ROOTS * p], dall[r - 1, ROOTS * p + 1])
                 for root in range(ROOTS):
                     ksend[r - 1, p, root] = mats[root].astype(BF16)
-        for r in (2, 1, 3):
-            k_copy(r, h).start()
-        return carry
-
-    lax.fori_loop(0, CHUNKS, k_chunk, 0)
+            k_copy(r, chunk).start()
+            return carry
+
+        lax.fori_loop(h * CHUNKS // 2, (h + 1) * CHUNKS // 2, body, 0)
+
+    ring(1, 0)
+    ring(1, 1)
+    wait_panels(2)
+    ring(2, 0)
+    grams(2)
+    ring(2, 1)
+    wait_panels(1)
+    ring(3, 0)
+    grams(1)
+    ring(3, 1)
+    ring(4, 0)
+    k_part(2, 0)
+    k_part(1, 0)
+    wait_panels(3)
+    grams(3)
+    ring(4, 1)
+    k_part(3, 0)
+    k_part(2, 1)
+    k_part(1, 1)
+    k_part(3, 1)
     wait_panels(0)
-    grams(0)
-
-    def own_chunk(h, carry):
+
+    def z_copy(k, h):
+        some = pl.ds(h * per, per)
+        to = (z + k) % NZ
+        return pltpu.make_async_remote_copy(
+            src_ref=sig_b.at[some, :, pl.ds(pl.multiple_of(to * piece, piece), piece), :],
+            dst_ref=zrecv.at[k, some],
+            send_sem=zs_sem.at[k, h],
+            recv_sem=zr_sem.at[k, h],
+            device_id=(pos, to),
+            device_id_type=MESH,
+        )
+
+    row_at = lax.broadcasted_iota(jnp.int32, (rank, rank), 0)
+    col_at = lax.broadcasted_iota(jnp.int32, (rank, rank), 1)
+
+    def sigma_chunk(h, carry):
+        for n in range(per):
+            gram_of(0, h * per + n)
         for n in range(per):
             p = h * per + n
             mats = k_of(0, p, transforms[ROOTS * p], transforms[ROOTS * p + 1])
             for root in range(ROOTS):
                 kown[p, root] = mats[root]
-        return carry
-
-    lax.fori_loop(0, CHUNKS, own_chunk, 0)
-
-    def z_copy(k, h):
-        some = pl.ds(h * per, per)
-        to = (z + k) % NZ
-        return pltpu.make_async_remote_copy(
-            src_ref=sig_b.at[some, :, pl.ds(pl.multiple_of(to * piece, piece), piece), :],
-            dst_ref=zrecv.at[k, some],
-            send_sem=zs_sem.at[k, h],
-            recv_sem=zr_sem.at[k, h],
-            device_id=(pos, to),
-            device_id_type=MESH,
-        )
-
-    row_at = lax.broadcasted_iota(jnp.int32, (rank, rank), 0)
-    col_at = lax.broadcasted_iota(jnp.int32, (rank, rank), 1)
-
-    def sigma_chunk(h, carry):
         for r in range(1, 4):
             k_copy(r, h).wait_recv()
         for n in range(per):
@@ -290,10 +308,21 @@
         return carry
 
     lax.fori_loop(0, CHUNKS, sigma_chunk, 0)
+    for r in ORDER:
+        for k in range(len(dests)):
+            panel_copy(*dests[k], r, k).wait_send()
+    for r in range(1, 4):
+        d_copy(r).wait_send()
+        for h in range(CHUNKS):
+            k_copy(r, h).wait_send()
+    for step in range(NZ // 2):
+        for way in (1, -1):
+            for h in range(2):
+                ring_copy(way, step, h).wait_send()
 
     def sum_chunk(h, carry):
         for k in range(1, NZ):
-            z_copy(k, h).wait_recv()
+            z_copy(k, h).wait()
         for n in range(per):
             p = h * per + n
             for root in range(ROOTS):
@@ -304,20 +333,6 @@
         return carry
 
     lax.fori_loop(0, CHUNKS, sum_chunk, 0)
-
-    for r in ORDER:
-        for k in range(len(dests)):
-            panel_copy(*dests[k], r, k).wait_send()
-    for r in range(1, 4):
-        d_copy(r).wait_send()
-    for step in range(NZ // 2):
-        for way in (1, -1):
-            ring_copy(way, step).wait_send()
-    for h in range(CHUNKS):
-        for r in range(1, 4):
-            k_copy(r, h).wait_send()
-        for k in range(1, NZ):
-            z_copy(k, h).wait_send()
 
 
 def per_device(panels, domain, pair_slots, ranks, transforms, trial):
@@ -360,10 +375,10 @@
             dma((4,)),
             dma((4,)),
             dma((4,)),
-            dma((4,)),
-            dma((4,)),
-            dma((4,)),
-            dma((4,)),
+            dma((4, 2)),
+            dma((4, 2)),
+            dma((4, 2)),
+            dma((4, 2)),
             dma((3, CHUNKS)),
             dma((3, CHUNKS)),
             dma((NZ, CHUNKS)),

time: 120 us -> 105 us (0.88)
  Pallas kernels: 118 us -> 103 us
    pallas_call x1, Pallas kernels: 118 us -> 103 us  [per_device(): pl.pallas_call(kernel, name='sigma', out_shape=jax.ShapeDtypeStruct((pair...]
where the time goes in v3:
time: 105 us
  Pallas kernels  103 us (98%)
  local copies, waits for them, and re-layouts  1.54 us (1%)
    pallas_call x1, Pallas kernels, per_device(): pl.pallas_call(kernel, name='sigma', out_shape=jax.ShapeDtypeStruct((pair...  103 us

profile of v3, /device:TPU:1, one launch (start us, length us, event | category | flops | bytes accessed | tf_op | source)
XLA Modules:
  0.0 104.6 jit_solution(3514424638526034557)
XLA Ops:
  0.0 103.1 %sigma.1 = bf16[12,2,16,128]{3,2,1,0:T(8,128)(2,1)} custom-call(s32[6,32]{1,0:T(8,128)} %bitcast.5, s32[2,12]{1,0:T(2,128)} %bitcast.6, s32[2,12]{1,0:T(2,128)} %bitcast.7, bf16[64,112,256]{2,1,0:T(8,128)(2,1)} %panels_in.1, bf16[24,256,128]{2,1,0:T(8,128)(2,1)} %bitcast.4, bf16[12,2,128,128]{3,2,1,0:T(8,128)(2,1)} %trial_in.1), custom_call_target="tpu_custom_call" | custom-call | tf_op jit(solution)/shard_map/sigma/pallas_call | solution.py:346
  103.1 1.5 %copy.8 = bf16[12,2,16,128]{3,2,1,0:T(8,128)(2,1)} copy(bf16[12,2,16,128]{3,2,1,0:T(8,128)(2,1)} %sigma.1) | data formatting | bytes 196608

commit v4 on v3

--- a/solution.py
+++ b/solution.py
@@ -10,7 +10,8 @@
 ROOTS = 2
 ORDER = (2, 1, 3, 0)
 CHUNKS = 6
-UNROLL = 3
+QUARTERS = 4
+EARLY = 2
 F32, BF16 = jnp.float32, jnp.bfloat16
 PLAIN = (((1,), (0,)), ((), ()))
 TRANS_A = (((0,), (0,)), ((), ()))
@@ -31,9 +32,9 @@
     panels, transforms, trial,
     recv0, recv1, recv2, recv3, stage, slots_v, slots_s, dall, gram,
     kown, ksend, krecv, sig_f, sig_b, zrecv,
-    in_sem, send_sem, recv_sem, slot_send, slot_recv, slot_local,
-    ds_sem, dr_sem, rs_sem, rr_sem, ls_sem, lr_sem,
-    ks_sem, kr_sem, zs_sem, zr_sem,
+    out_v, in_sem, send_sem, recv_sem, slot_send, slot_recv, slot_local,
+    ds_sem, dr_sem, ring_sem, rr_sem, lr_sem,
+    ks_sem, kr_sem, zs_sem, zr_sem, out_sem,
 ):
     pairs, piece, rank = out.shape[0], out.shape[2], out.shape[3]
     rows = panels.shape[1]
@@ -43,6 +44,9 @@
     pos = lax.axis_index("pairs")
     z = lax.axis_index("aux")
     x, y, c = pos // (2 * NY), (pos // 2) % NY, pos % 2
+
+    def arrived(ref, sem):
+        pltpu.make_async_copy(ref, ref, sem).wait()
 
     loads = [
         pltpu.make_async_copy(src, dst, in_sem.at[n])
@@ -96,8 +100,8 @@
         return pltpu.make_async_remote_copy(
             src_ref=stage.at[k, r],
             dst_ref=recvs[r].at[:, pl.ds(block * rows, rows), :],
-            send_sem=send_sem.at[r, k],
-            recv_sem=recv_sem.at[r, k],
+            send_sem=send_sem,
+            recv_sem=recv_sem.at[r],
             device_id=(place(*dest), z),
             device_id_type=MESH,
         )
@@ -121,25 +125,25 @@
         return pltpu.make_async_remote_copy(
             src_ref=transforms.at[:, part_of(z), :],
             dst_ref=dall.at[r - 1, :, part_of(z), :],
-            send_sem=ds_sem.at[r],
-            recv_sem=dr_sem.at[r],
+            send_sem=ds_sem,
+            recv_sem=dr_sem,
             device_id=(place(*peer(NX - r)), z),
             device_id_type=MESH,
         )
 
-    half = pairs * ROOTS // 2
+    quarter = pairs // QUARTERS
 
     def ring_copy(way, step, h):
         origin = part_of(z - way * step + NZ)
         chosen = slice(None)
         if step == NZ // 2 - 1:
             chosen = pl.ds(0, 2) if way == 1 else pl.ds(2, 1)
-        send, recv = (rs_sem, rr_sem) if way == 1 else (ls_sem, lr_sem)
-        ref = dall.at[chosen, pl.ds(h * half, half), origin, :]
+        recv = rr_sem if way == 1 else lr_sem
+        ref = dall.at[chosen, pl.ds(h * quarter * ROOTS, quarter * ROOTS), origin, :]
         return pltpu.make_async_remote_copy(
             src_ref=ref,
             dst_ref=ref,
-            send_sem=send.at[step, h],
+            send_sem=ring_sem,
             recv_sem=recv.at[step, h],
             device_id=(pos, (z + way + NZ) % NZ),
             device_id_type=MESH,
@@ -169,28 +173,26 @@
         group = group_of((x, y, c), r)
         for s in range(lslot):
             recvs[r][s, 0:rows, :] = panels[domain[s, group]]
-    for r in range(1, 4):
-        d_copy(r).wait_recv()
+    arrived(dall.at[:, :, part_of(z), :], dr_sem)
     ring(0, 0)
     ring(0, 1)
     for r, k in work:
         if dests[k][1] % 2 == 0:
             panel_copy(*dests[k], r, k).start()
-    locals_ = [
-        pltpu.make_async_copy(slots_v.at[r] if r else slots_in, slots_s.at[r], slot_local.at[r])
-        for r in range(4)
-    ]
-    for r in range(4):
-        if r:
-            slot_copy(r).wait()
-        locals_[r].start()
-    for local in locals_:
-        local.wait()
+    mine = pltpu.make_async_copy(slots_in, slots_s.at[0], slot_local.at[0])
+    theirs = pltpu.make_async_copy(
+        slots_v.at[pl.ds(1, 3)], slots_s.at[pl.ds(1, 3)], slot_local.at[1]
+    )
+    mine.start()
+    for r in range(1, 4):
+        slot_copy(r).wait()
+    theirs.start()
+    theirs.wait()
+    mine.wait()
     loads[2].wait()
 
     def wait_panels(r):
-        for k in range(len(dests)):
-            panel_copy(*dests[k], r, k).wait_recv()
+        arrived(recvs[r].at[:, pl.ds(rows, 7 * rows), :], recv_sem.at[r])
 
     def gram_of(r, p):
         left = recvs[r][slots_s[r, 0, p]]
@@ -199,11 +201,11 @@
 
     def grams(r):
         def body(n, carry):
-            for u in range(UNROLL):
-                gram_of(r, n * UNROLL + u)
+            for u in range(quarter):
+                gram_of(r, n * quarter + u)
             return carry
 
-        lax.fori_loop(0, pairs // UNROLL, body, 0)
+        lax.fori_loop(0, QUARTERS, body, 0)
 
     def k_of(r, p, d0, d1):
         g_high, g_low = split(gram[r, p])
@@ -224,45 +226,65 @@
         return pltpu.make_async_remote_copy(
             src_ref=ksend.at[r - 1, some],
             dst_ref=krecv.at[r - 1, some],
-            send_sem=ks_sem.at[r - 1, h],
-            recv_sem=kr_sem.at[r - 1, h],
+            send_sem=ks_sem,
+            recv_sem=kr_sem.at[h],
             device_id=(place(*peer(r)), z),
             device_id_type=MESH,
         )
 
-    def k_part(r, h):
-        def body(chunk, carry):
-            for n in range(per):
-                p = chunk * per + n
+    def k_part(r, first, count=1):
+        def body(q, carry):
+            for n in range(quarter):
+                p = q * quarter + n
                 mats = k_of(r, p, dall[r - 1, ROOTS * p], dall[r - 1, ROOTS * p + 1])
                 for root in range(ROOTS):
                     ksend[r - 1, p, root] = mats[root].astype(BF16)
-            k_copy(r, chunk).start()
             return carry
 
-        lax.fori_loop(h * CHUNKS // 2, (h + 1) * CHUNKS // 2, body, 0)
+        lax.fori_loop(first, first + count, body, 0)
+
+    def k_send(first, last):
+        for h in range(first, last):
+            for r in (2, 1, 3):
+                k_copy(r, h).start()
 
     ring(1, 0)
     ring(1, 1)
+    ring(2, 0)
+    ring(2, 1)
+    ring(3, 0)
+    ring(0, 2)
     wait_panels(2)
-    ring(2, 0)
     grams(2)
-    ring(2, 1)
-    wait_panels(1)
-    ring(3, 0)
-    grams(1)
     ring(3, 1)
+    ring(0, 3)
     ring(4, 0)
     k_part(2, 0)
-    k_part(1, 0)
+    ring(1, 2)
+    ring(4, 1)
+    k_part(2, 1)
+    ring(1, 3)
+    wait_panels(1)
+    ring(2, 2)
+    grams(1)
+    ring(2, 3)
+    k_part(1, 0, 2)
+    ring(3, 2)
+    ring(3, 3)
+    ring(4, 2)
+    k_part(2, 2)
     wait_panels(3)
     grams(3)
-    ring(4, 1)
-    k_part(3, 0)
-    k_part(2, 1)
-    k_part(1, 1)
-    k_part(3, 1)
+    k_part(3, 0, 2)
+    k_send(0, EARLY)
+    k_part(1, 2)
+    k_part(3, 2)
+    ring(4, 3)
+    k_part(2, 3)
+    k_part(1, 3)
+    k_part(3, 3)
     wait_panels(0)
+    k_send(EARLY, CHUNKS)
 
     def z_copy(k, h):
         some = pl.ds(h * per, per)
@@ -270,8 +292,8 @@
         return pltpu.make_async_remote_copy(
             src_ref=sig_b.at[some, :, pl.ds(pl.multiple_of(to * piece, piece), piece), :],
             dst_ref=zrecv.at[k, some],
-            send_sem=zs_sem.at[k, h],
-            recv_sem=zr_sem.at[k, h],
+            send_sem=zs_sem,
+            recv_sem=zr_sem.at[h],
             device_id=(pos, to),
             device_id_type=MESH,
         )
@@ -287,8 +309,7 @@
             mats = k_of(0, p, transforms[ROOTS * p], transforms[ROOTS * p + 1])
             for root in range(ROOTS):
                 kown[p, root] = mats[root]
-        for r in range(1, 4):
-            k_copy(r, h).wait_recv()
+        arrived(krecv.at[:, pl.ds(h * per, per)], kr_sem.at[h])
         for n in range(per):
             p = h * per + n
             for root in range(ROOTS):
@@ -308,31 +329,29 @@
         return carry
 
     lax.fori_loop(0, CHUNKS, sigma_chunk, 0)
-    for r in ORDER:
-        for k in range(len(dests)):
-            panel_copy(*dests[k], r, k).wait_send()
-    for r in range(1, 4):
-        d_copy(r).wait_send()
-        for h in range(CHUNKS):
-            k_copy(r, h).wait_send()
-    for step in range(NZ // 2):
-        for way in (1, -1):
-            for h in range(2):
-                ring_copy(way, step, h).wait_send()
+    arrived(stage, send_sem)
+    arrived(dall.at[:, :, part_of(z), :], ds_sem)
+    arrived(dall.at[:, :, pl.ds(0, (NZ - 1) * part), :], ring_sem)
+    arrived(ksend, ks_sem)
+
+    def out_copy(some):
+        return pltpu.make_async_copy(out_v.at[some], out.at[some], out_sem)
 
     def sum_chunk(h, carry):
-        for k in range(1, NZ):
-            z_copy(k, h).wait()
+        arrived(zrecv.at[pl.ds(1, NZ - 1), pl.ds(h * per, per)], zr_sem.at[h])
         for n in range(per):
             p = h * per + n
             for root in range(ROOTS):
                 total = sig_f[p, root, pl.ds(pl.multiple_of(z * piece, piece), piece), :]
                 for k in range(1, NZ):
                     total = total + zrecv[k, p, root].astype(F32)
-                out[p, root] = total.astype(BF16)
+                out_v[p, root] = total.astype(BF16)
+        out_copy(pl.ds(h * per, per)).start()
         return carry
 
     lax.fori_loop(0, CHUNKS, sum_chunk, 0)
+    arrived(zrecv.at[pl.ds(1, NZ - 1)], zs_sem)
+    arrived(out_v, out_sem)
 
 
 def per_device(panels, domain, pair_slots, ranks, transforms, trial):
@@ -348,7 +367,7 @@
         name="sigma",
         out_shape=jax.ShapeDtypeStruct((pairs, roots, rank // NZ, rank), BF16),
         in_specs=[smem, smem, vmem, far, far, far],
-        out_specs=vmem,
+        out_specs=far,
         scratch_shapes=[
             pltpu.VMEM((occ, rows, width), BF16),
             pltpu.VMEM((pairs * roots, width, rank), BF16),
@@ -367,22 +386,23 @@
             pltpu.VMEM((pairs, roots, rank, rank), F32),
             pltpu.VMEM((pairs, roots, rank, rank), BF16),
             pltpu.VMEM((NZ, pairs, roots, rank // NZ, rank), BF16),
+            pltpu.VMEM((pairs, roots, rank // NZ, rank), BF16),
             dma((3,)),
-            dma((4, 7)),
-            dma((4, 7)),
+            dma,
             dma((4,)),
             dma((4,)),
             dma((4,)),
-            dma((4,)),
-            dma((4,)),
-            dma((4, 2)),
-            dma((4, 2)),
-            dma((4, 2)),
-            dma((4, 2)),
-            dma((3, CHUNKS)),
-            dma((3, CHUNKS)),
-            dma((NZ, CHUNKS)),
-            dma((NZ, CHUNKS)),
+            dma((2,)),
+            dma,
+            dma,
+            dma,
+            dma((NZ // 2, QUARTERS)),
+            dma((NZ // 2, QUARTERS)),
+            dma,
+            dma((CHUNKS,)),
+            dma,
+            dma((CHUNKS,)),
+            dma,
         ],
         compiler_params=pltpu.CompilerParams(
             collective_id=0, has_side_effects=True, vmem_limit_bytes=67043328

time: 105 us -> 102 us (0.971)
  Pallas kernels: 103 us -> 100 us
    pallas_call x1, Pallas kernels: 103 us -> 100 us  [per_device(): pl.pallas_call(kernel, name='sigma', out_shape=jax.ShapeDtypeStruct((pair...]
where the time goes in v4:
time: 102 us
  Pallas kernels  100 us (98%)
  local copies, waits for them, and re-layouts  1.54 us (2%)
    pallas_call x1, Pallas kernels, per_device(): pl.pallas_call(kernel, name='sigma', out_shape=jax.ShapeDtypeStruct((pair...  100 us

profile of v4, /device:TPU:1, one launch (start us, length us, event | category | flops | bytes accessed | tf_op | source)
XLA Modules:
  0.0 101.7 jit_solution(14514626393180883710)
XLA Ops:
  0.0 100.2 %sigma.1 = bf16[12,2,16,128]{3,2,1,0:T(8,128)(2,1)} custom-call(s32[6,32]{1,0:T(8,128)} %bitcast.5, s32[2,12]{1,0:T(2,128)} %bitcast.6, s32[2,12]{1,0:T(2,128)} %bitcast.7, bf16[64,112,256]{2,1,0:T(8,128)(2,1)} %panels_in.1, bf16[24,256,128]{2,1,0:T(8,128)(2,1)} %bitcast.4, bf16[12,2,128,128]{3,2,1,0:T(8,128)(2,1)} %trial_in.1), custom_call_target="tpu_custom_call" | custom-call | tf_op jit(solution)/shard_map/sigma/pallas_call | solution.py:365
  100.2 1.5 %copy.8 = bf16[12,2,16,128]{3,2,1,0:T(8,128)(2,1)} copy(bf16[12,2,16,128]{3,2,1,0:T(8,128)(2,1)} %sigma.1) | data formatting | bytes 196608

commit v5 on v4

--- a/solution.py
+++ b/solution.py
@@ -9,9 +9,7 @@
 NX, NY, NZ = 4, 4, 8
 ROOTS = 2
 ORDER = (2, 1, 3, 0)
-CHUNKS = 6
 QUARTERS = 4
-EARLY = 2
 F32, BF16 = jnp.float32, jnp.bfloat16
 PLAIN = (((1,), (0,)), ((), ()))
 TRANS_A = (((0,), (0,)), ((), ()))
@@ -28,13 +26,13 @@
 
 
 def kernel(
-    domain, ranks, slots_in, panels_in, transforms_in, trial_in, out,
-    panels, transforms, trial,
+    domain_in, ranks_in, slots_in, panels_in, transforms_in, trial_in, out,
+    domain, ranks, panels, transforms, trial,
     recv0, recv1, recv2, recv3, stage, slots_v, slots_s, dall, gram,
-    kown, ksend, krecv, sig_f, sig_b, zrecv,
+    keep_f, swap_out, swap_in, ysend, yrecv, sig_f, sig_b, zrecv,
     out_v, in_sem, send_sem, recv_sem, slot_send, slot_recv, slot_local,
     ds_sem, dr_sem, ring_sem, rr_sem, lr_sem,
-    ks_sem, kr_sem, zs_sem, zr_sem, out_sem,
+    ws_sem, wr_sem, ys_sem, yr_sem, zs_sem, zr_sem, out_sem,
 ):
     pairs, piece, rank = out.shape[0], out.shape[2], out.shape[3]
     rows = panels.shape[1]
@@ -47,15 +45,6 @@
 
     def arrived(ref, sem):
         pltpu.make_async_copy(ref, ref, sem).wait()
-
-    loads = [
-        pltpu.make_async_copy(src, dst, in_sem.at[n])
-        for n, (src, dst) in enumerate(
-            ((panels_in, panels), (transforms_in, transforms), (trial_in, trial))
-        )
-    ]
-    for load in loads:
-        load.start()
 
     def place(x2, y2, c2):
         return (x2 % NX) * (2 * NY) + (y2 % NY) * 2 + c2
@@ -88,6 +77,17 @@
         pl.semaphore_signal(barrier, inc=1, device_id=target, device_id_type=MESH)
         greeted += 1
 
+    def load(src, dst, n):
+        copy = pltpu.make_async_copy(src, dst, in_sem.at[n])
+        copy.start()
+        return copy
+
+    slot_load = load(slots_in, slots_v.at[0], 0)
+    domain_load = load(domain_in, domain, 1)
+    transforms_load = load(transforms_in, transforms, 2)
+    panels_load = load(panels_in, panels, 3)
+    late_loads = load(ranks_in, ranks, 4), load(trial_in, trial, 5)
+
     dests = [(same(m), 2 * m) for m in range(1, 4)] + [(other(m), 2 * m + 1) for m in range(4)]
     dests = [dests[k] for k in (1, 5, 0, 2, 4, 6, 3)]
 
@@ -108,7 +108,7 @@
 
     def slot_copy(r):
         return pltpu.make_async_remote_copy(
-            src_ref=slots_in,
+            src_ref=slots_v.at[0],
             dst_ref=slots_v.at[r],
             send_sem=slot_send.at[r],
             recv_sem=slot_recv.at[r],
@@ -157,13 +157,15 @@
                 ring_copy(way, step, h).start()
 
     work = [(r, k) for r in ORDER for k in range(len(dests))]
-    loads[1].wait()
+    slot_load.wait()
+    transforms_load.wait()
+    domain_load.wait()
     pl.semaphore_wait(barrier, greeted)
     for r in (2, 1, 3):
         d_copy(r).start()
     for r in range(1, 4):
         slot_copy(r).start()
-    loads[0].wait()
+    panels_load.wait()
     for r, k in work:
         fill(dests[k][0], r, k)
     for r, k in work:
@@ -179,17 +181,13 @@
     for r, k in work:
         if dests[k][1] % 2 == 0:
             panel_copy(*dests[k], r, k).start()
-    mine = pltpu.make_async_copy(slots_in, slots_s.at[0], slot_local.at[0])
-    theirs = pltpu.make_async_copy(
-        slots_v.at[pl.ds(1, 3)], slots_s.at[pl.ds(1, 3)], slot_local.at[1]
-    )
-    mine.start()
     for r in range(1, 4):
         slot_copy(r).wait()
-    theirs.start()
-    theirs.wait()
-    mine.wait()
-    loads[2].wait()
+    to_smem = pltpu.make_async_copy(slots_v, slots_s, slot_local)
+    to_smem.start()
+    to_smem.wait()
+    for copy in late_loads:
+        copy.wait()
 
     def wait_panels(r):
         arrived(recvs[r].at[:, pl.ds(rows, 7 * rows), :], recv_sem.at[r])
@@ -219,34 +217,67 @@
             result.append(summed[:, :rank] + summed[:, rank:])
         return result
 
-    per = pairs // CHUNKS
-
-    def k_copy(r, h):
-        some = pl.ds(h * per, per)
-        return pltpu.make_async_remote_copy(
-            src_ref=ksend.at[r - 1, some],
-            dst_ref=krecv.at[r - 1, some],
-            send_sem=ks_sem,
-            recv_sem=kr_sem.at[h],
+    side = (z + c) % 2
+    partner = (z + 1 - 2 * side + NZ) % NZ
+
+    def pair_at(chunk, mine, n):
+        owner = side if mine else 1 - side
+        return (2 * chunk + owner) * quarter + n
+
+    def chunk_of(chunk):
+        return pl.ds(chunk * quarter, quarter)
+
+    def swap_copy(r, chunk):
+        return pltpu.make_async_remote_copy(
+            src_ref=swap_out.at[r, chunk_of(chunk)],
+            dst_ref=swap_in.at[r, chunk_of(chunk)],
+            send_sem=ws_sem,
+            recv_sem=wr_sem.at[r, chunk],
+            device_id=(pos, partner),
+            device_id_type=MESH,
+        )
+
+    def y_copy(r, chunk):
+        return pltpu.make_async_remote_copy(
+            src_ref=ysend.at[r - 1, chunk_of(chunk)],
+            dst_ref=yrecv.at[r - 1, chunk_of(chunk)],
+            send_sem=ys_sem,
+            recv_sem=yr_sem.at[chunk],
             device_id=(place(*peer(r)), z),
             device_id_type=MESH,
         )
 
-    def k_part(r, first, count=1):
-        def body(q, carry):
-            for n in range(quarter):
-                p = q * quarter + n
-                mats = k_of(r, p, dall[r - 1, ROOTS * p], dall[r - 1, ROOTS * p + 1])
-                for root in range(ROOTS):
-                    ksend[r - 1, p, root] = mats[root].astype(BF16)
-            return carry
-
-        lax.fori_loop(first, first + count, body, 0)
-
-    def k_send(first, last):
-        for h in range(first, last):
-            for r in (2, 1, 3):
-                k_copy(r, h).start()
+    def k_quarter(r, chunk, mine):
+        for n in range(quarter):
+            p = pair_at(chunk, mine, n)
+            source = dall.at[r - 1] if r else transforms
+            mats = k_of(r, p, source[ROOTS * p], source[ROOTS * p + 1])
+            for root in range(ROOTS):
+                if mine:
+                    keep_f[r, chunk * quarter + n, root] = mats[root]
+                else:
+                    swap_out[r, chunk * quarter + n, root] = mats[root].astype(BF16)
+
+    def k_both(r, chunk):
+        k_quarter(r, chunk, False)
+        swap_copy(r, chunk).start()
+        k_quarter(r, chunk, True)
+
+    def own(chunk, mine):
+        for n in range(quarter):
+            gram_of(0, pair_at(chunk, mine, n))
+        k_quarter(0, chunk, mine)
+        if not mine:
+            swap_copy(0, chunk).start()
+
+    def merge(r, chunk):
+        swap_copy(r, chunk).wait_recv()
+        for n in range(quarter):
+            at = chunk * quarter + n
+            for root in range(ROOTS):
+                summed = keep_f[r, at, root] + swap_in[r, at, root].astype(F32)
+                ysend[r - 1, at, root] = summed.astype(BF16)
+        y_copy(r, chunk).start()
 
     ring(1, 0)
     ring(1, 1)
@@ -259,41 +290,43 @@
     ring(3, 1)
     ring(0, 3)
     ring(4, 0)
-    k_part(2, 0)
     ring(1, 2)
     ring(4, 1)
-    k_part(2, 1)
     ring(1, 3)
+    k_both(2, 0)
     wait_panels(1)
     ring(2, 2)
     grams(1)
     ring(2, 3)
-    k_part(1, 0, 2)
+    k_both(1, 0)
     ring(3, 2)
     ring(3, 3)
-    ring(4, 2)
-    k_part(2, 2)
     wait_panels(3)
     grams(3)
-    k_part(3, 0, 2)
-    k_send(0, EARLY)
-    k_part(1, 2)
-    k_part(3, 2)
+    ring(4, 2)
+    k_both(3, 0)
     ring(4, 3)
-    k_part(2, 3)
-    k_part(1, 3)
-    k_part(3, 3)
+    k_both(2, 1)
+    k_both(1, 1)
+    k_both(3, 1)
+    merge(2, 0)
+    merge(1, 0)
+    merge(3, 0)
     wait_panels(0)
-    k_send(EARLY, CHUNKS)
-
-    def z_copy(k, h):
-        some = pl.ds(h * per, per)
+    own(0, False)
+    own(1, False)
+    merge(2, 1)
+    merge(1, 1)
+    merge(3, 1)
+    own(0, True)
+
+    def z_copy(k, chunk):
         to = (z + k) % NZ
         return pltpu.make_async_remote_copy(
-            src_ref=sig_b.at[some, :, pl.ds(pl.multiple_of(to * piece, piece), piece), :],
-            dst_ref=zrecv.at[k, some],
+            src_ref=sig_b.at[chunk_of(chunk), :, pl.ds(pl.multiple_of(to * piece, piece), piece), :],
+            dst_ref=zrecv.at[k, chunk_of(chunk)],
             send_sem=zs_sem,
-            recv_sem=zr_sem.at[h],
+            recv_sem=zr_sem.at[chunk],
             device_id=(pos, to),
             device_id_type=MESH,
         )
@@ -301,55 +334,54 @@
     row_at = lax.broadcasted_iota(jnp.int32, (rank, rank), 0)
     col_at = lax.broadcasted_iota(jnp.int32, (rank, rank), 1)
 
-    def sigma_chunk(h, carry):
-        for n in range(per):
-            gram_of(0, h * per + n)
-        for n in range(per):
-            p = h * per + n
-            mats = k_of(0, p, transforms[ROOTS * p], transforms[ROOTS * p + 1])
+    def sigmas(chunk):
+        swap_copy(0, chunk).wait_recv()
+        arrived(yrecv.at[:, chunk_of(chunk)], yr_sem.at[chunk])
+        for n in range(quarter):
+            at = chunk * quarter + n
+            p = pair_at(chunk, True, n)
             for root in range(ROOTS):
-                kown[p, root] = mats[root]
-        arrived(krecv.at[:, pl.ds(h * per, per)], kr_sem.at[h])
-        for n in range(per):
-            p = h * per + n
-            for root in range(ROOTS):
-                kmat = kown[p, root]
+                kmat = keep_f[0, at, root] + swap_in[0, at, root].astype(F32)
                 for r in range(1, 4):
-                    kmat = kmat + krecv[r - 1, p, root].astype(F32)
+                    kmat = kmat + yrecv[r - 1, at, root].astype(F32)
                 keep = (row_at < ranks[root, p]) & (col_at < ranks[root, p])
                 kmat = jnp.where(keep, kmat, 0.0)
                 amp = jnp.where(keep, trial[p, root].astype(F32), 0.0).astype(BF16)
                 both = jnp.concatenate(split(kmat), axis=1)
                 sig = kmat + dot(both, jnp.concatenate([amp, amp], axis=0))
                 sig = sig + dot(jnp.concatenate([amp, amp], axis=1), both, TRANS_B)
-                sig_f[p, root] = sig
-                sig_b[p, root] = sig.astype(BF16)
+                sig_f[at, root] = sig
+                sig_b[at, root] = sig.astype(BF16)
         for k in (4, 3, 5, 2, 6, 1, 7):
-            z_copy(k, h).start()
-        return carry
-
-    lax.fori_loop(0, CHUNKS, sigma_chunk, 0)
+            z_copy(k, chunk).start()
+
+    sigmas(0)
+    own(1, True)
+    sigmas(1)
     arrived(stage, send_sem)
     arrived(dall.at[:, :, part_of(z), :], ds_sem)
     arrived(dall.at[:, :, pl.ds(0, (NZ - 1) * part), :], ring_sem)
-    arrived(ksend, ks_sem)
-
-    def out_copy(some):
+    arrived(swap_out, ws_sem)
+    arrived(ysend, ys_sem)
+
+    def out_copy(chunk):
+        some = pl.ds(chunk * 2 * quarter, 2 * quarter)
         return pltpu.make_async_copy(out_v.at[some], out.at[some], out_sem)
 
-    def sum_chunk(h, carry):
-        arrived(zrecv.at[pl.ds(1, NZ - 1), pl.ds(h * per, per)], zr_sem.at[h])
-        for n in range(per):
-            p = h * per + n
+    for chunk in range(2):
+        arrived(zrecv.at[pl.ds(1, NZ - 1), chunk_of(chunk)], zr_sem.at[chunk])
+        for n in range(quarter):
+            at = chunk * quarter + n
             for root in range(ROOTS):
-                total = sig_f[p, root, pl.ds(pl.multiple_of(z * piece, piece), piece), :]
-                for k in range(1, NZ):
-                    total = total + zrecv[k, p, root].astype(F32)
-                out_v[p, root] = total.astype(BF16)
-        out_copy(pl.ds(h * per, per)).start()
-        return carry
-
-    lax.fori_loop(0, CHUNKS, sum_chunk, 0)
+                total = sig_f[at, root, pl.ds(pl.multiple_of(z * piece, piece), piece), :]
+                for k in range(2, NZ, 2):
+                    total = total + zrecv[k, at, root].astype(F32)
+                out_v[pair_at(chunk, True, n), root] = total.astype(BF16)
+                total = zrecv[1, at, root].astype(F32)
+                for k in range(3, NZ, 2):
+                    total = total + zrecv[k, at, root].astype(F32)
+                out_v[pair_at(chunk, False, n), root] = total.astype(BF16)
+        out_copy(chunk).start()
     arrived(zrecv.at[pl.ds(1, NZ - 1)], zs_sem)
     arrived(out_v, out_sem)
 
@@ -358,17 +390,18 @@
     pairs, roots, width, rank = transforms.shape
     occ, rows, _ = panels.shape
     lslot = domain.shape[1]
-    smem = pl.BlockSpec(memory_space=pltpu.SMEM)
-    vmem = pl.BlockSpec(memory_space=pltpu.VMEM)
+    half = pairs // 2
     far = pl.BlockSpec(memory_space=pl.ANY)
     dma = pltpu.SemaphoreType.DMA
     return pl.pallas_call(
         kernel,
         name="sigma",
         out_shape=jax.ShapeDtypeStruct((pairs, roots, rank // NZ, rank), BF16),
-        in_specs=[smem, smem, vmem, far, far, far],
+        in_specs=[far] * 6,
         out_specs=far,
         scratch_shapes=[
+            pltpu.SMEM(domain.shape[::-1], jnp.int32),
+            pltpu.SMEM((roots, pairs), jnp.int32),
             pltpu.VMEM((occ, rows, width), BF16),
             pltpu.VMEM((pairs * roots, width, rank), BF16),
             pltpu.VMEM((pairs, roots, rank, rank), BF16),
@@ -380,28 +413,32 @@
             pltpu.SMEM((4, 2, pairs), jnp.int32),
             pltpu.VMEM((3, pairs * roots, width, rank), BF16),
             pltpu.VMEM((4, pairs, width, width), F32),
-            pltpu.VMEM((pairs, roots, rank, rank), F32),
-            pltpu.VMEM((3, pairs, roots, rank, rank), BF16),
-            pltpu.VMEM((3, pairs, roots, rank, rank), BF16),
-            pltpu.VMEM((pairs, roots, rank, rank), F32),
-            pltpu.VMEM((pairs, roots, rank, rank), BF16),
-            pltpu.VMEM((NZ, pairs, roots, rank // NZ, rank), BF16),
+            pltpu.VMEM((4, half, roots, rank, rank), F32),
+            pltpu.VMEM((4, half, roots, rank, rank), BF16),
+            pltpu.VMEM((4, half, roots, rank, rank), BF16),
+            pltpu.VMEM((3, half, roots, rank, rank), BF16),
+            pltpu.VMEM((3, half, roots, rank, rank), BF16),
+            pltpu.VMEM((half, roots, rank, rank), F32),
+            pltpu.VMEM((half, roots, rank, rank), BF16),
+            pltpu.VMEM((NZ, half, roots, rank // NZ, rank), BF16),
             pltpu.VMEM((pairs, roots, rank // NZ, rank), BF16),
-            dma((3,)),
+            dma((6,)),
             dma,
             dma((4,)),
             dma((4,)),
             dma((4,)),
-            dma((2,)),
+            dma,
             dma,
             dma,
             dma,
             dma((NZ // 2, QUARTERS)),
             dma((NZ // 2, QUARTERS)),
             dma,
-            dma((CHUNKS,)),
-            dma,
-            dma((CHUNKS,)),
+            dma((4, 2)),
+            dma,
+            dma((2,)),
+            dma,
+            dma((2,)),
             dma,
         ],
         compiler_params=pltpu.CompilerParams(

time: 102 us -> 96.7 us (0.948)
  Pallas kernels: 100 us -> 95.1 us
    pallas_call x1, Pallas kernels: 100 us -> 95.1 us  [per_device(): pl.pallas_call(kernel, name='sigma', out_shape=jax.ShapeDtypeStruct((pair...]
where the time goes in v5:
time: 96.7 us; the launch traced here: 96.6 us
  Pallas kernels  95.1 us (98%)
  local copies, waits for them, and re-layouts  1.54 us (2%)
    pallas_call x1, Pallas kernels, per_device(): pl.pallas_call(kernel, name='sigma', out_shape=jax.ShapeDtypeStruct((pair...  95.1 us

profile of v5, /device:TPU:1, one launch (start us, length us, event | category | flops | bytes accessed | tf_op | source)
XLA Modules:
  0.0 96.6 jit_solution(7434015783124022115)
XLA Ops:
  0.0 95.1 %sigma.1 = bf16[12,2,16,128]{3,2,1,0:T(8,128)(2,1)} custom-call(s32[6,32]{1,0:T(8,128)} %bitcast.5, s32[2,12]{1,0:T(2,128)} %bitcast.6, s32[2,12]{1,0:T(2,128)} %bitcast.7, bf16[64,112,256]{2,1,0:T(8,128)(2,1)} %panels_in.1, bf16[24,256,128]{2,1,0:T(8,128)(2,1)} %bitcast.4, bf16[12,2,128,128]{3,2,1,0:T(8,128)(2,1)} %trial_in.1), custom_call_target="tpu_custom_call" | custom-call | tf_op jit(solution)/shard_map/sigma/pallas_call | solution.py:396
  95.1 1.5 %copy.8 = bf16[12,2,16,128]{3,2,1,0:T(8,128)(2,1)} copy(bf16[12,2,16,128]{3,2,1,0:T(8,128)(2,1)} %sigma.1) | data formatting | bytes 196608

commit v6 on v5

--- a/solution.py
+++ b/solution.py
@@ -28,7 +28,7 @@
 def kernel(
     domain_in, ranks_in, slots_in, panels_in, transforms_in, trial_in, out,
     domain, ranks, panels, transforms, trial,
-    recv0, recv1, recv2, recv3, stage, slots_v, slots_s, dall, gram,
+    recv0, recv1, recv2, recv3, stage, slots_v, slots_s, dall, gram, half_t,
     keep_f, swap_out, swap_in, ysend, yrecv, sig_f, sig_b, zrecv,
     out_v, in_sem, send_sem, recv_sem, slot_send, slot_recv, slot_local,
     ds_sem, dr_sem, ring_sem, rr_sem, lr_sem,
@@ -205,18 +205,6 @@
 
         lax.fori_loop(0, QUARTERS, body, 0)
 
-    def k_of(r, p, d0, d1):
-        g_high, g_low = split(gram[r, p])
-        coeffs = jnp.concatenate([d0, d1], axis=1)
-        t_high, t_low = split(dot(g_high, coeffs) + dot(g_low, coeffs))
-        result = []
-        for root, d in enumerate((d0, d1)):
-            cols = slice(root * rank, (root + 1) * rank)
-            both = jnp.concatenate([t_high[:, cols], t_low[:, cols]], axis=1)
-            summed = dot(d, both, TRANS_A)
-            result.append(summed[:, :rank] + summed[:, rank:])
-        return result
-
     side = (z + c) % 2
     partner = (z + 1 - 2 * side + NZ) % NZ
 
@@ -247,26 +235,36 @@
             device_id_type=MESH,
         )
 
-    def k_quarter(r, chunk, mine):
-        for n in range(quarter):
+    def k_quarters(r, quarters):
+        source = dall.at[r - 1] if r else transforms
+        todo = [(chunk, mine, n) for chunk, mine in quarters for n in range(quarter)]
+        for slot, (chunk, mine, n) in enumerate(todo):
             p = pair_at(chunk, mine, n)
-            source = dall.at[r - 1] if r else transforms
-            mats = k_of(r, p, source[ROOTS * p], source[ROOTS * p + 1])
+            coeffs = jnp.concatenate([source[ROOTS * p], source[ROOTS * p + 1]], axis=1)
+            g_high, g_low = split(gram[r, p])
+            t_high, t_low = split(dot(g_high, coeffs) + dot(g_low, coeffs))
             for root in range(ROOTS):
+                cols = slice(root * rank, (root + 1) * rank)
+                half_t[slot, root, :, 0:rank] = t_high[:, cols]
+                half_t[slot, root, :, rank : 2 * rank] = t_low[:, cols]
+        for slot, (chunk, mine, n) in enumerate(todo):
+            p = pair_at(chunk, mine, n)
+            for root in range(ROOTS):
+                summed = dot(source[ROOTS * p + root], half_t[slot, root], TRANS_A)
+                mat = summed[:, :rank] + summed[:, rank:]
                 if mine:
-                    keep_f[r, chunk * quarter + n, root] = mats[root]
+                    keep_f[r, chunk * quarter + n, root] = mat
                 else:
-                    swap_out[r, chunk * quarter + n, root] = mats[root].astype(BF16)
+                    swap_out[r, chunk * quarter + n, root] = mat.astype(BF16)
 
     def k_both(r, chunk):
-        k_quarter(r, chunk, False)
+        k_quarters(r, [(chunk, False), (chunk, True)])
         swap_copy(r, chunk).start()
-        k_quarter(r, chunk, True)
 
     def own(chunk, mine):
         for n in range(quarter):
             gram_of(0, pair_at(chunk, mine, n))
-        k_quarter(0, chunk, mine)
+        k_quarters(0, [(chunk, mine)])
         if not mine:
             swap_copy(0, chunk).start()
 
@@ -309,16 +307,17 @@
     k_both(2, 1)
     k_both(1, 1)
     k_both(3, 1)
+    wait_panels(0)
     merge(2, 0)
     merge(1, 0)
     merge(3, 0)
-    wait_panels(0)
     own(0, False)
     own(1, False)
     merge(2, 1)
     merge(1, 1)
     merge(3, 1)
     own(0, True)
+    own(1, True)
 
     def z_copy(k, chunk):
         to = (z + k) % NZ
@@ -356,7 +355,6 @@
             z_copy(k, chunk).start()
 
     sigmas(0)
-    own(1, True)
     sigmas(1)
     arrived(stage, send_sem)
     arrived(dall.at[:, :, part_of(z), :], ds_sem)
@@ -376,11 +374,11 @@
                 total = sig_f[at, root, pl.ds(pl.multiple_of(z * piece, piece), piece), :]
                 for k in range(2, NZ, 2):
                     total = total + zrecv[k, at, root].astype(F32)
-                out_v[pair_at(chunk, True, n), root] = total.astype(BF16)
+                out_v[pair_at(chunk, True, n), root] = total
                 total = zrecv[1, at, root].astype(F32)
                 for k in range(3, NZ, 2):
                     total = total + zrecv[k, at, root].astype(F32)
-                out_v[pair_at(chunk, False, n), root] = total.astype(BF16)
+                out_v[pair_at(chunk, False, n), root] = total
         out_copy(chunk).start()
     arrived(zrecv.at[pl.ds(1, NZ - 1)], zs_sem)
     arrived(out_v, out_sem)
@@ -396,7 +394,7 @@
     return pl.pallas_call(
         kernel,
         name="sigma",
-        out_shape=jax.ShapeDtypeStruct((pairs, roots, rank // NZ, rank), BF16),
+        out_shape=jax.ShapeDtypeStruct((pairs, roots, rank // NZ, rank), F32),
         in_specs=[far] * 6,
         out_specs=far,
         scratch_shapes=[
@@ -413,6 +411,7 @@
             pltpu.SMEM((4, 2, pairs), jnp.int32),
             pltpu.VMEM((3, pairs * roots, width, rank), BF16),
             pltpu.VMEM((4, pairs, width, width), F32),
+            pltpu.VMEM((half, roots, width, 2 * rank), BF16),
             pltpu.VMEM((4, half, roots, rank, rank), F32),
             pltpu.VMEM((4, half, roots, rank, rank), BF16),
             pltpu.VMEM((4, half, roots, rank, rank), BF16),
@@ -421,7 +420,7 @@
             pltpu.VMEM((half, roots, rank, rank), F32),
             pltpu.VMEM((half, roots, rank, rank), BF16),
             pltpu.VMEM((NZ, half, roots, rank // NZ, rank), BF16),
-            pltpu.VMEM((pairs, roots, rank // NZ, rank), BF16),
+            pltpu.VMEM((pairs, roots, rank // NZ, rank), F32),
             dma((6,)),
             dma,
             dma((4,)),
@@ -451,7 +450,7 @@
         panels,
         transforms.reshape(pairs * roots, width, rank),
         trial,
-    )
+    ).astype(BF16)
 
 
 def solution(mesh):

time: 96.7 us -> 96.7 us (level)
  other arithmetic: 0 us -> 1.58 us
  local copies, waits for them, and re-layouts: 1.54 us -> 0 us
    convert_element_type x0 -> x1, other arithmetic: none -> 1.58 us  [per_device(): return pl.pallas_call(kernel, name='sigma', out_shape=jax.ShapeDtypeStruc...]
    unnamed x1 -> x0, local copies, waits for them, and re-layouts: 1.54 us -> none
where the time goes in v6:
time: 96.7 us; the launch traced here: 96.6 us
  Pallas kernels  95.1 us (98%)
  other arithmetic  1.58 us (2%)
    pallas_call x1, Pallas kernels, per_device(): pl.pallas_call(kernel, name='sigma', out_shape=jax.ShapeDtypeStruct((pair...  95.1 us

profile of v6, /device:TPU:1, one launch (start us, length us, event | category | flops | bytes accessed | tf_op | source)
XLA Modules:
  0.0 96.6 jit_solution(7512121021581925110)
XLA Ops:
  0.0 95.1 %sigma.1 = f32[12,2,16,128]{3,2,1,0:T(8,128)} custom-call(s32[6,32]{1,0:T(8,128)} %bitcast.5, s32[2,12]{1,0:T(2,128)} %bitcast.6, s32[2,12]{1,0:T(2,128)} %bitcast.7, bf16[64,112,256]{2,1,0:T(8,128)(2,1)} %panels_in.1, bf16[24,256,128]{2,1,0:T(8,128)(2,1)} %bitcast.4, bf16[12,2,128,128]{3,2,1,0:T(8,128)(2,1)} %trial_in.1), custom_call_target="tpu_custom_call" | custom-call | tf_op jit(solution)/shard_map/sigma/pallas_call | solution.py:394
  95.1 1.6 %convert_element_type.3 = bf16[12,2,16,128]{3,2,1,0:T(8,128)(2,1)} convert(f32[12,2,16,128]{3,2,1,0:T(8,128)} %sigma.1) | non-fusion elementwise | flops 49152 | bytes 294912 | tf_op jit(solution)/shard_map/convert_element_type | solution.py:453
